TPU v7x, 32 devices: a whole 2x2x4 slice. The times are simulated.
32 devices in a mesh: cols: 4 (over y, x), dom: 8 (over z, core).
Axes of the slice: x: 2, y: 2, z: 4, core: 2. Of those that a mesh axis runs over, the one named last changes fastest.
Arguments:
- features: bfloat16 [768, 4096], P('cols', 'dom'), may hold values from -6 to 6
- proj_in: bfloat16 [768, 256], P('cols'), may hold values from -0.3125 to 0.3125
- self_weight: bfloat16 [256, 256], replicated, may hold values from -0.375 to 0.375
- neigh_weight: bfloat16 [256, 256], replicated, may hold values from -0.375 to 0.375
- neighbors: int32 [16, 4096], P(None, 'dom'), may hold values from 0 to 1023, as said below
- degree: int32 [4096], P('dom'), may hold values from 1 to 16
- send_rows: int32 [8, 512], P('dom'), may hold values from 0 to 511
- send_count: int32 [8, 8], P('dom'), may hold values from 0 to 64, as said below
Outputs:
- layer_out: bfloat16 [256, 4096], P('cols', 'dom')
Inputs may be any that keep to these rules, and one draw needn't show every extreme that they name: `neighbors`: A code at or above 512 names a source partition other than the node's own and a slot below send_count of that source towards the node's partition. Every partition's rows are received in full (64 slots) from every other partition for at least one partition in every draw. `send_count`: zero on the diagonal; elsewhere 1 to 64, and 64 from every source towards at least one partition.
All inputs are finite; a program needn't handle non-finite values.
Results may differ from a plain program's by a relative error of at most 0.0051.
Values may be sent and summed in bfloat16 or wider, within the bound.
A program may use at most 64 MiB of HBM per device.

v0:
```python
import functools
import math

import jax
import jax.numpy as jnp
from jax import lax
from jax.experimental import pallas as pl
from jax.experimental.pallas import tpu as pltpu
from jax.sharding import PartitionSpec as P

MESH = pl.DeviceIdType.MESH
LANES = 128


def dot(left, right, left_dim, right_dim):
    return lax.dot_general(
        left, right, (((left_dim,), (right_dim,)), ((), ())), preferred_element_type=jnp.float32
    )


def kernel(
    cols,
    parts,
    capacity,
    feat_hbm,
    proj_hbm,
    selfw_hbm,
    neighw_hbm,
    neigh_hbm,
    degree_hbm,
    rows_hbm,
    count_hbm,
    out_ref,
    feat,
    proj,
    selfw,
    neighw,
    neigh,
    degree,
    rows,
    count,
    own,
    outgoing_sum,
    incoming_sum,
    hidden_all,
    mean_all,
    pick,
    packed_out,
    packed_in,
    table,
    counts,
    in_sem,
    sum_send,
    sum_recv,
    row_send,
    row_recv,
    hid_send,
    hid_recv,
    mean_send,
    mean_recv,
):
    column = lax.axis_index("cols")
    part = lax.axis_index("dom")
    width = out_ref.shape[0]
    nodes = out_ref.shape[1]
    hid = width * cols
    slots = rows.shape[1]
    slot_count = neigh.shape[0]
    fold = LANES // capacity
    short = width // fold

    loads = [
        pltpu.make_async_copy(source, target, in_sem.at[i])
        for i, (source, target) in enumerate(
            (
                (feat_hbm, feat),
                (proj_hbm, proj),
                (rows_hbm, rows),
                (count_hbm, count),
                (neigh_hbm, neigh),
                (degree_hbm, degree),
                (selfw_hbm, selfw),
                (neighw_hbm, neighw),
            )
        )
    ]
    for load in loads:
        load.start()

    barrier = pltpu.get_barrier_semaphore()
    for step in range(1, cols):
        pl.semaphore_signal(
            barrier, inc=1, device_id=((column + step) % cols, part), device_id_type=MESH
        )

    def greet(step, carry):
        pl.semaphore_signal(
            barrier, inc=1, device_id=(column, (part + step) % parts), device_id_type=MESH
        )
        return carry

    lax.fori_loop(1, parts, greet, 0)

    loads[0].wait()
    loads[1].wait()
    partial_value = dot(proj[...], feat[...], 0, 0)
    own[...] = partial_value
    outgoing_sum[...] = partial_value.astype(outgoing_sum.dtype)
    pl.semaphore_wait(barrier, cols + parts - 2)

    def band(index):
        return pl.ds(pl.multiple_of(index * width, width), width)

    def to_column(source, target, send, recv, step):
        peer = (column + step) % cols
        return pltpu.make_async_remote_copy(
            src_ref=source,
            dst_ref=target,
            send_sem=send.at[step - 1],
            recv_sem=recv.at[step - 1],
            device_id=(peer, part),
            device_id_type=MESH,
        )

    sums = [
        to_column(
            outgoing_sum.at[band((column + step) % cols)],
            incoming_sum.at[step - 1],
            sum_send,
            sum_recv,
            step,
        )
        for step in range(1, cols)
    ]
    for copy in sums:
        copy.start()

    for load in loads[2:]:
        load.wait()
    group = min(slots, 512)
    spread = group * fold

    def choose(index, carry):
        start = pl.multiple_of(index * group, group)
        wanted = rows[:, pl.ds(start, group)]
        source = (
            lax.broadcasted_iota(jnp.int32, (parts, group), 1) + start
        ) // capacity == lax.broadcasted_iota(jnp.int32, (parts, group), 0)
        amount = dot(
            jnp.broadcast_to(count[...].astype(jnp.float32), (8, parts)).astype(jnp.bfloat16),
            source.astype(jnp.float32).astype(jnp.bfloat16),
            1,
            0,
        )[0:1, :]
        slot = (lax.broadcasted_iota(jnp.int32, (1, group), 1) % capacity).astype(jnp.float32)
        wanted = jnp.where(slot < amount, wanted, -1)
        pieces = []
        for block in range(group // capacity):
            piece = wanted[:, block * capacity : (block + 1) * capacity]
            pieces += [piece] * fold
        wide = jnp.concatenate(pieces, axis=1)
        hit = lax.broadcasted_iota(jnp.int32, (nodes, spread), 0) == wide
        pick[:, pl.ds(pl.multiple_of(index * spread, spread), spread)] = jnp.where(
            hit, 1.0, 0.0
        ).astype(jnp.bfloat16)
        return carry

    lax.fori_loop(0, slots // group, choose, 0)

    used = lax.broadcasted_iota(jnp.int32, (slot_count, nodes), 0) < degree[...]
    codes = jnp.where(used, neigh[...], -1)
    neigh[...] = codes
    depth = 256
    row_of = lax.broadcasted_iota(jnp.int32, (depth, LANES), 0).astype(jnp.float32).astype(jnp.bfloat16)
    one = jnp.ones((depth, LANES), jnp.bfloat16)
    zero = jnp.zeros((depth, LANES), jnp.bfloat16)

    def tally(index, carry):
        start = pl.multiple_of(index * depth, depth)
        for lane in range(nodes // LANES):
            there = slice(lane * LANES, (lane + 1) * LANES)
            near = jnp.clip(neigh[:, there] - start, -1, depth).astype(jnp.float32)
            total = zero
            for slot in range(slot_count):
                code = jnp.broadcast_to(near[slot : slot + 1, :], (16, LANES)).astype(jnp.bfloat16)
                code = jnp.concatenate([code] * (depth // 16), axis=0)
                total = total + jnp.where(row_of == code, one, zero)
            counts[pl.ds(start, depth), there] = total
        return carry

    lax.fori_loop(0, counts.shape[0] // depth, tally, 0)

    mine = (
        lax.broadcasted_iota(jnp.int32, (width, hid), 0) + column * width
        == lax.broadcasted_iota(jnp.int32, (width, hid), 1)
    )
    mine = jnp.where(mine, 1.0, 0.0).astype(jnp.bfloat16)
    self_rows = dot(mine, selfw[...], 1, 1).astype(jnp.bfloat16)
    neigh_rows = dot(mine, neighw[...], 1, 1).astype(jnp.bfloat16)

    total = own[band(column), :]
    for step in range(1, cols):
        sums[step - 1].wait_recv()
    for step in range(1, cols):
        total = total + incoming_sum[step - 1].astype(jnp.float32)
    hidden = total.astype(jnp.bfloat16)
    hidden_all[band(column), :] = hidden

    folded = lax.broadcasted_iota(jnp.int32, (short, spread), 1) % LANES // capacity

    def pack(index, carry):
        start = pl.multiple_of(index * spread, spread)
        chosen = dot(hidden_all[band(column), :], pick[:, pl.ds(start, spread)], 1, 0)
        tight = chosen[0:short, :]
        for piece in range(1, fold):
            tight = jnp.where(folded == piece, chosen[piece * short : (piece + 1) * short, :], tight)
        tight = tight.astype(jnp.bfloat16)
        for block in range(spread // LANES):
            packed_out[index * (spread // LANES) + block] = tight[:, block * LANES : (block + 1) * LANES]
        return carry

    lax.fori_loop(0, slots // group, pack, 0)

    def to_part(step):
        peer = (part + step) % parts
        return pltpu.make_async_remote_copy(
            src_ref=packed_out.at[peer],
            dst_ref=packed_in.at[part],
            send_sem=row_send.at[step],
            recv_sem=row_recv.at[step],
            device_id=(column, peer),
            device_id_type=MESH,
        )

    def send_rows(step, carry):
        to_part(step).start()
        return carry

    lax.fori_loop(1, parts, send_rows, 0)

    def share(buffer, send, recv):
        return [
            to_column(buffer.at[band(column)], buffer.at[band(column)], send, recv, step)
            for step in range(1, cols)
        ]

    hidden_copies = share(hidden_all, hid_send, hid_recv)
    for copy in hidden_copies:
        copy.start()

    packed_in[part] = jnp.zeros((short, LANES), jnp.bfloat16)
    local_sum = dot(hidden, counts[0:nodes, :], 1, 0)

    def arrive(step, carry):
        to_part(step).wait_recv()
        return carry

    lax.fori_loop(1, parts, arrive, 0)

    half = lax.broadcasted_iota(jnp.int32, (short, LANES), 1) // capacity

    def unpack(index, carry):
        for piece in range(fold):
            value = jnp.zeros((short, LANES), jnp.float32)
            for place in range(fold):
                block = packed_in[index * fold + place].astype(jnp.float32)
                shift = (place - piece) * capacity % LANES
                if shift:
                    block = pltpu.roll(block, shift, 1)
                value = jnp.where(half == place, block, value)
            table[piece * short : (piece + 1) * short, pl.ds(pl.multiple_of(index * LANES, LANES), LANES)] = (
                value.astype(jnp.bfloat16)
            )
        return carry

    lax.fori_loop(0, parts // fold, unpack, 0)
    summed = local_sum + dot(table[...], counts[nodes:, :], 1, 0)
    mean_all[band(column), :] = (summed / degree[...].astype(jnp.float32)).astype(jnp.bfloat16)
    mean_copies = share(mean_all, mean_send, mean_recv)
    for copy in mean_copies:
        copy.start()
    for copy in hidden_copies:
        copy.wait_recv()
    result = dot(self_rows, hidden_all[...], 1, 0)
    for copy in mean_copies:
        copy.wait_recv()
    result = result + dot(neigh_rows, mean_all[...], 1, 0)
    out_ref[...] = jnp.maximum(result, 0.0).astype(out_ref.dtype)

    for copy in sums + hidden_copies + mean_copies:
        copy.wait_send()

    def sent(step, carry):
        to_part(step).wait_send()
        return carry

    lax.fori_loop(1, parts, sent, 0)


def local(features, proj_in, self_weight, neigh_weight, neighbors, degree, send_rows, send_count):
    cols = lax.axis_size("cols")
    parts = lax.axis_size("dom")
    hid = proj_in.shape[1]
    width = hid // cols
    nodes = features.shape[1]
    slots = send_rows.shape[1]
    capacity = slots // parts
    fold = LANES // capacity
    short = width // fold
    degree = degree.reshape(1, nodes)
    arguments = (
        features,
        proj_in,
        self_weight,
        neigh_weight,
        neighbors,
        degree,
        send_rows,
        send_count,
    )
    bf16 = jnp.bfloat16
    copies = pltpu.SemaphoreType.DMA
    return pl.pallas_call(
        functools.partial(kernel, cols, parts, capacity),
        out_shape=jax.ShapeDtypeStruct((width, nodes), bf16),
        in_specs=[pl.BlockSpec(memory_space=pltpu.HBM)] * len(arguments),
        out_specs=pl.BlockSpec(memory_space=pltpu.VMEM),
        scratch_shapes=[pltpu.VMEM(a.shape, a.dtype) for a in arguments]
        + [
            pltpu.VMEM((hid, nodes), jnp.float32),
            pltpu.VMEM((hid, nodes), bf16),
            pltpu.VMEM((cols - 1, width, nodes), bf16),
            pltpu.VMEM((hid, nodes), bf16),
            pltpu.VMEM((hid, nodes), bf16),
            pltpu.VMEM((nodes, slots * fold), bf16),
            pltpu.VMEM((parts, short, LANES), bf16),
            pltpu.VMEM((parts, short, LANES), bf16),
            pltpu.VMEM((width, slots), bf16),
            pltpu.VMEM((nodes + slots, nodes), bf16),
            copies((len(arguments),)),
            copies((cols - 1,)),
            copies((cols - 1,)),
            copies((parts,)),
            copies((parts,)),
            copies((cols - 1,)),
            copies((cols - 1,)),
            copies((cols - 1,)),
            copies((cols - 1,)),
        ],
        compiler_params=pltpu.CompilerParams(
            collective_id=0, has_side_effects=True, vmem_limit_bytes=67043328
        ),
        name="layer",
    )(*arguments)


def solution(mesh):
    return jax.shard_map(
        local,
        mesh=mesh,
        in_specs=(
            P("cols", "dom"),
            P("cols", None),
            P(),
            P(),
            P(None, "dom"),
            P("dom"),
            P("dom", None),
            P("dom", None),
        ),
        out_specs=P("cols", "dom"),
        check_vma=False,
    )
```

profile of v0, /device:TPU:0, one launch (start us, length us, event | category | flops | bytes accessed | tf_op | source)
XLA Modules:
  0.0 22.1 jit_solution(1054490766892522131)
XLA Ops:
  0.0 20.6 %layer.1 = bf16[64,512]{1,0:T(8,128)(2,1)} custom-call(bf16[192,512]{1,0:T(8,128)(2,1)} %feat_hbm.1, bf16[192,256]{1,0:T(8,128)(2,1)} %proj_hbm.1, bf16[256,256]{1,0:T(8,128)(2,1)} %selfw_hbm.1, bf16[256,256]{1,0:T(8,128)(2,1)} %neighw_hbm.1, s32[16,512]{1,0:T(8,128)} %neigh_hbm.1, s32[1,512]{1,0:T(1,128)} %bitcast.1, s32[1,512]{1,0:T(1,128)} %rows_hbm.1, ...), custom_call_target="tpu_custom_call" | custom-call | tf_op jit(solution)/shard_map/layer/pallas_call | solution.py:323
  20.6 1.5 %copy.10 = bf16[64,512]{1,0:T(8,128)(2,1)} copy(bf16[64,512]{1,0:T(8,128)(2,1)} %layer.1) | data formatting | bytes 131072
where the time goes:
time: 22.3 us; the launch traced here: 22.1 us
  Pallas kernels  20.6 us (92%)
  local copies, waits for them, and re-layouts  1.47 us (7%)
    pallas_call x1, Pallas kernels, local(): pl.pallas_call(functools.partial(kernel, cols, parts, capacity), out_shap...  20.6 us
    unnamed x1, local copies, waits for them, and re-layouts  1.47 us

commit v1 on v0

--- a/solution.py
+++ b/solution.py
@@ -40,10 +40,12 @@
     rows,
     count,
     own,
+    own_self,
     outgoing_sum,
+    outgoing_self,
     incoming_sum,
-    hidden_all,
-    mean_all,
+    incoming_self,
+    reduced,
     pick,
     packed_out,
     packed_in,
@@ -54,10 +56,8 @@
     sum_recv,
     row_send,
     row_recv,
-    hid_send,
-    hid_recv,
-    mean_send,
-    mean_recv,
+    self_send,
+    self_recv,
 ):
     column = lax.axis_index("cols")
     part = lax.axis_index("dom")
@@ -75,12 +75,12 @@
             (
                 (feat_hbm, feat),
                 (proj_hbm, proj),
+                (neighw_hbm, neighw),
+                (selfw_hbm, selfw),
                 (rows_hbm, rows),
                 (count_hbm, count),
                 (neigh_hbm, neigh),
                 (degree_hbm, degree),
-                (selfw_hbm, selfw),
-                (neighw_hbm, neighw),
             )
         )
     ]
@@ -101,41 +101,66 @@
 
     lax.fori_loop(1, parts, greet, 0)
 
-    loads[0].wait()
-    loads[1].wait()
-    partial_value = dot(proj[...], feat[...], 0, 0)
-    own[...] = partial_value
-    outgoing_sum[...] = partial_value.astype(outgoing_sum.dtype)
+    for load in loads[:3]:
+        load.wait()
+    to_neigh = dot(proj[...], neighw[...], 1, 0).astype(jnp.bfloat16)
+    value = dot(to_neigh, feat[...], 0, 0)
+    own[...] = value
+    outgoing_sum[...] = value.astype(outgoing_sum.dtype)
     pl.semaphore_wait(barrier, cols + parts - 2)
 
     def band(index):
         return pl.ds(pl.multiple_of(index * width, width), width)
 
-    def to_column(source, target, send, recv, step):
-        peer = (column + step) % cols
-        return pltpu.make_async_remote_copy(
-            src_ref=source,
-            dst_ref=target,
-            send_sem=send.at[step - 1],
-            recv_sem=recv.at[step - 1],
-            device_id=(peer, part),
-            device_id_type=MESH,
-        )
-
-    sums = [
-        to_column(
-            outgoing_sum.at[band((column + step) % cols)],
-            incoming_sum.at[step - 1],
-            sum_send,
-            sum_recv,
-            step,
-        )
-        for step in range(1, cols)
-    ]
+    def other(step, me, count):
+        return step - 1 + (step - 1 + count - me) // count
+
+    def scatter(outgoing, incoming, send, recv):
+        copies = []
+        for step in range(1, cols):
+            peer = other(step, column, cols)
+            copies.append(
+                pltpu.make_async_remote_copy(
+                    src_ref=outgoing.at[band(peer)],
+                    dst_ref=incoming.at[column],
+                    send_sem=send.at[step - 1],
+                    recv_sem=recv.at[column],
+                    device_id=(peer, part),
+                    device_id_type=MESH,
+                )
+            )
+        return copies
+
+    def arrivals(outgoing, incoming, send, recv):
+        copies = []
+        for step in range(1, cols):
+            peer = other(step, column, cols)
+            copies.append(
+                pltpu.make_async_remote_copy(
+                    src_ref=outgoing.at[band(peer)],
+                    dst_ref=incoming.at[peer],
+                    send_sem=send.at[step - 1],
+                    recv_sem=recv.at[peer],
+                    device_id=(peer, part),
+                    device_id_type=MESH,
+                )
+            )
+        return copies
+
+    sums = scatter(outgoing_sum, incoming_sum, sum_send, sum_recv)
     for copy in sums:
         copy.start()
 
-    for load in loads[2:]:
+    loads[3].wait()
+    to_self = dot(proj[...], selfw[...], 1, 0).astype(jnp.bfloat16)
+    value = dot(to_self, feat[...], 0, 0)
+    own_self[...] = value
+    outgoing_self[...] = value.astype(outgoing_self.dtype)
+    selves = scatter(outgoing_self, incoming_self, self_send, self_recv)
+    for copy in selves:
+        copy.start()
+
+    for load in loads[4:]:
         load.wait()
     group = min(slots, 512)
     spread = group * fold
@@ -190,27 +215,22 @@
 
     lax.fori_loop(0, counts.shape[0] // depth, tally, 0)
 
-    mine = (
-        lax.broadcasted_iota(jnp.int32, (width, hid), 0) + column * width
-        == lax.broadcasted_iota(jnp.int32, (width, hid), 1)
-    )
-    mine = jnp.where(mine, 1.0, 0.0).astype(jnp.bfloat16)
-    self_rows = dot(mine, selfw[...], 1, 1).astype(jnp.bfloat16)
-    neigh_rows = dot(mine, neighw[...], 1, 1).astype(jnp.bfloat16)
-
-    total = own[band(column), :]
-    for step in range(1, cols):
-        sums[step - 1].wait_recv()
-    for step in range(1, cols):
-        total = total + incoming_sum[step - 1].astype(jnp.float32)
-    hidden = total.astype(jnp.bfloat16)
-    hidden_all[band(column), :] = hidden
+    def total_of(mine, copies, incoming):
+        for copy in copies:
+            copy.wait_recv()
+        total = mine[band(column), :]
+        for step in range(1, cols):
+            total = total + incoming[other(step, column, cols)].astype(jnp.float32)
+        return total
+
+    total = total_of(own, arrivals(outgoing_sum, incoming_sum, sum_send, sum_recv), incoming_sum)
+    reduced[...] = total.astype(jnp.bfloat16)
 
     folded = lax.broadcasted_iota(jnp.int32, (short, spread), 1) % LANES // capacity
 
     def pack(index, carry):
         start = pl.multiple_of(index * spread, spread)
-        chosen = dot(hidden_all[band(column), :], pick[:, pl.ds(start, spread)], 1, 0)
+        chosen = dot(reduced[...], pick[:, pl.ds(start, spread)], 1, 0)
         tight = chosen[0:short, :]
         for piece in range(1, fold):
             tight = jnp.where(folded == piece, chosen[piece * short : (piece + 1) * short, :], tight)
@@ -222,37 +242,38 @@
     lax.fori_loop(0, slots // group, pack, 0)
 
     def to_part(step):
-        peer = (part + step) % parts
+        peer = other(step, part, parts)
         return pltpu.make_async_remote_copy(
             src_ref=packed_out.at[peer],
             dst_ref=packed_in.at[part],
             send_sem=row_send.at[step],
-            recv_sem=row_recv.at[step],
+            recv_sem=row_recv.at[part],
             device_id=(column, peer),
             device_id_type=MESH,
         )
 
+    def from_part(step):
+        peer = other(step, part, parts)
+        return pltpu.make_async_remote_copy(
+            src_ref=packed_out.at[peer],
+            dst_ref=packed_in.at[peer],
+            send_sem=row_send.at[step],
+            recv_sem=row_recv.at[peer],
+            device_id=(column, peer),
+            device_id_type=MESH,
+        )
+
     def send_rows(step, carry):
         to_part(step).start()
         return carry
 
     lax.fori_loop(1, parts, send_rows, 0)
 
-    def share(buffer, send, recv):
-        return [
-            to_column(buffer.at[band(column)], buffer.at[band(column)], send, recv, step)
-            for step in range(1, cols)
-        ]
-
-    hidden_copies = share(hidden_all, hid_send, hid_recv)
-    for copy in hidden_copies:
-        copy.start()
-
     packed_in[part] = jnp.zeros((short, LANES), jnp.bfloat16)
-    local_sum = dot(hidden, counts[0:nodes, :], 1, 0)
+    local_sum = dot(reduced[...], counts[0:nodes, :], 1, 0)
 
     def arrive(step, carry):
-        to_part(step).wait_recv()
+        from_part(step).wait_recv()
         return carry
 
     lax.fori_loop(1, parts, arrive, 0)
@@ -275,19 +296,13 @@
 
     lax.fori_loop(0, parts // fold, unpack, 0)
     summed = local_sum + dot(table[...], counts[nodes:, :], 1, 0)
-    mean_all[band(column), :] = (summed / degree[...].astype(jnp.float32)).astype(jnp.bfloat16)
-    mean_copies = share(mean_all, mean_send, mean_recv)
-    for copy in mean_copies:
-        copy.start()
-    for copy in hidden_copies:
-        copy.wait_recv()
-    result = dot(self_rows, hidden_all[...], 1, 0)
-    for copy in mean_copies:
-        copy.wait_recv()
-    result = result + dot(neigh_rows, mean_all[...], 1, 0)
+    result = summed / degree[...].astype(jnp.float32)
+    result = result + total_of(
+        own_self, arrivals(outgoing_self, incoming_self, self_send, self_recv), incoming_self
+    )
     out_ref[...] = jnp.maximum(result, 0.0).astype(out_ref.dtype)
 
-    for copy in sums + hidden_copies + mean_copies:
+    for copy in sums + selves:
         copy.wait_send()
 
     def sent(step, carry):
@@ -328,10 +343,12 @@
         scratch_shapes=[pltpu.VMEM(a.shape, a.dtype) for a in arguments]
         + [
             pltpu.VMEM((hid, nodes), jnp.float32),
-            pltpu.VMEM((hid, nodes), bf16),
-            pltpu.VMEM((cols - 1, width, nodes), bf16),
+            pltpu.VMEM((hid, nodes), jnp.float32),
             pltpu.VMEM((hid, nodes), bf16),
             pltpu.VMEM((hid, nodes), bf16),
+            pltpu.VMEM((cols, width, nodes), bf16),
+            pltpu.VMEM((cols, width, nodes), bf16),
+            pltpu.VMEM((width, nodes), bf16),
             pltpu.VMEM((nodes, slots * fold), bf16),
             pltpu.VMEM((parts, short, LANES), bf16),
             pltpu.VMEM((parts, short, LANES), bf16),
@@ -339,13 +356,11 @@
             pltpu.VMEM((nodes + slots, nodes), bf16),
             copies((len(arguments),)),
             copies((cols - 1,)),
-            copies((cols - 1,)),
+            copies((cols,)),
             copies((parts,)),
             copies((parts,)),
             copies((cols - 1,)),
-            copies((cols - 1,)),
-            copies((cols - 1,)),
-            copies((cols - 1,)),
+            copies((cols,)),
         ],
         compiler_params=pltpu.CompilerParams(
             collective_id=0, has_side_effects=True, vmem_limit_bytes=67043328

time: 22.3 us -> 18.2 us (0.82)
  Pallas kernels: 20.6 us -> 16.5 us
    pallas_call x1, Pallas kernels: 20.6 us -> 16.5 us  [local(): pl.pallas_call(functools.partial(kernel, cols, parts, capacity), out_shap...]
where the time goes in v1:
time: 18.2 us; the launch traced here: 18 us
  Pallas kernels  16.5 us (91%)
  local copies, waits for them, and re-layouts  1.47 us (8%)
    pallas_call x1, Pallas kernels, local(): pl.pallas_call(functools.partial(kernel, cols, parts, capacity), out_shap...  16.5 us
    unnamed x1, local copies, waits for them, and re-layouts  1.47 us

profile of v1, /device:TPU:0, one launch (start us, length us, event | category | flops | bytes accessed | tf_op | source)
XLA Modules:
  0.0 18.0 jit_solution(4881001997788773040)
XLA Ops:
  0.0 16.5 %layer.1 = bf16[64,512]{1,0:T(8,128)(2,1)} custom-call(bf16[192,512]{1,0:T(8,128)(2,1)} %feat_hbm.1, bf16[192,256]{1,0:T(8,128)(2,1)} %proj_hbm.1, bf16[256,256]{1,0:T(8,128)(2,1)} %selfw_hbm.1, bf16[256,256]{1,0:T(8,128)(2,1)} %neighw_hbm.1, s32[16,512]{1,0:T(8,128)} %neigh_hbm.1, s32[1,512]{1,0:T(1,128)} %bitcast.1, s32[1,512]{1,0:T(1,128)} %rows_hbm.1, ...), custom_call_target="tpu_custom_call" | custom-call | tf_op jit(solution)/shard_map/layer/pallas_call | solution.py:338
  16.5 1.5 %copy.10 = bf16[64,512]{1,0:T(8,128)(2,1)} copy(bf16[64,512]{1,0:T(8,128)(2,1)} %layer.1) | data formatting | bytes 131072

commit v2 on v1

--- a/solution.py
+++ b/solution.py
@@ -335,6 +335,7 @@
     )
     bf16 = jnp.bfloat16
     copies = pltpu.SemaphoreType.DMA
+    limit = (16 << 20) + (slots * nodes * (fold + 1) + hid * nodes * 16) * 2
     return pl.pallas_call(
         functools.partial(kernel, cols, parts, capacity),
         out_shape=jax.ShapeDtypeStruct((width, nodes), bf16),
@@ -363,10 +364,10 @@
             copies((cols,)),
         ],
         compiler_params=pltpu.CompilerParams(
-            collective_id=0, has_side_effects=True, vmem_limit_bytes=67043328
+            collective_id=0, has_side_effects=True, vmem_limit_bytes=limit
         ),
         name="layer",
-    )(*arguments)
+    )(*[pltpu.with_memory_space_constraint(a, pltpu.HBM) for a in arguments])
 
 
 def solution(mesh):

time: 18.2 us -> 16.7 us (0.918)
  local copies, waits for them, and re-layouts: 1.47 us -> 0.63 us
  Pallas kernels: 16.5 us -> 15.9 us
    unnamed x1, local copies, waits for them, and re-layouts: 1.47 us -> 0.63 us
    pallas_call x1, Pallas kernels: 16.5 us -> 15.9 us  [local(): pl.pallas_call(functools.partial(kernel, cols, parts, capacity), out_shap...]
where the time goes in v2:
time: 16.7 us; the launch traced here: 16.5 us
  Pallas kernels  15.9 us (95%)
  local copies, waits for them, and re-layouts  0.63 us (4%)
    pallas_call x1, Pallas kernels, local(): pl.pallas_call(functools.partial(kernel, cols, parts, capacity), out_shap...  15.9 us
    unnamed x1, local copies, waits for them, and re-layouts  0.63 us

profile of v2, /device:TPU:0, one launch (start us, length us, event | category | flops | bytes accessed | tf_op | source)
XLA Modules:
  0.0 16.5 jit_solution(8406194300727561237)
XLA Ops:
  0.0 15.9 %layer.1 = bf16[64,512]{1,0:T(8,128)(2,1)S(1)} custom-call(bf16[192,512]{1,0:T(8,128)(2,1)} %feat_hbm.1, bf16[192,256]{1,0:T(8,128)(2,1)} %proj_hbm.1, bf16[256,256]{1,0:T(8,128)(2,1)} %selfw_hbm.1, bf16[256,256]{1,0:T(8,128)(2,1)} %neighw_hbm.1, s32[16,512]{1,0:T(8,128)} %neigh_hbm.1, s32[1,512]{1,0:T(1,128)} %bitcast.1, s32[1,512]{1,0:T(1,128)} %rows_hbm.1, ...), custom_call_target="tpu_custom_call" | custom-call | tf_op jit(solution)/shard_map/layer/pallas_call | solution.py:339
  15.9 0.6 %copy.10 = bf16[64,512]{1,0:T(8,128)(2,1)} copy(bf16[64,512]{1,0:T(8,128)(2,1)S(1)} %layer.1) | data formatting | bytes 131072

commit v3 on v0

v3 whole, which is shorter than its diff:
```python
import functools

import jax
import jax.numpy as jnp
from jax import lax
from jax.experimental import pallas as pl
from jax.experimental.pallas import tpu as pltpu
from jax.sharding import PartitionSpec as P

MESH = pl.DeviceIdType.MESH
LANES = 128
CHUNKS = 4


def dot(left, right, left_dim, right_dim):
    return lax.dot_general(
        left, right, (((left_dim,), (right_dim,)), ((), ())), preferred_element_type=jnp.float32
    )


def partner(me, step, count):
    if count & (count - 1):
        return (me + step) % count
    other = me
    for bit in range(count.bit_length()):
        if step >> bit & 1:
            size = 1 << bit
            other = other + size - 2 * size * (me // size % 2)
    return other


def kernel(
    cols,
    parts,
    capacity,
    feat_hbm,
    proj_hbm,
    selfw_hbm,
    neighw_hbm,
    neigh_hbm,
    degree_hbm,
    rows_hbm,
    count_hbm,
    out_ref,
    feat,
    proj,
    selfw,
    neighw,
    neigh,
    degree,
    rows,
    count,
    weights,
    weights_self,
    projected,
    own,
    own_self,
    outgoing_sum,
    outgoing_self,
    incoming_sum,
    incoming_self,
    pick,
    packed_out,
    packed_in,
    remote,
    counts,
    in_sem,
    sum_send,
    sum_recv,
    row_send,
    row_recv,
    self_send,
    self_recv,
):
    column = lax.axis_index("cols")
    part = lax.axis_index("dom")
    width = out_ref.shape[0]
    nodes = out_ref.shape[1]
    slots = rows.shape[1]
    slot_count = neigh.shape[0]
    fold = LANES // capacity
    short = width // fold
    pairs = parts // fold
    steps = sorted(range(1, cols), key=lambda step: -bin(step).count("1"))

    loads = [
        pltpu.make_async_copy(source, target, in_sem.at[i])
        for i, (source, target) in enumerate(
            (
                (rows_hbm, rows),
                (count_hbm, count),
                (neighw_hbm, neighw),
                (proj_hbm, proj),
                (feat_hbm, feat),
                (selfw_hbm, selfw),
                (neigh_hbm, neigh),
                (degree_hbm, degree),
            )
        )
    ]
    for load in loads:
        load.start()

    barrier = pltpu.get_barrier_semaphore()
    for step in range(1, cols):
        pl.semaphore_signal(
            barrier, inc=1, device_id=((column + step) % cols, part), device_id_type=MESH
        )

    def greet(step, carry):
        pl.semaphore_signal(
            barrier, inc=1, device_id=(column, (part + step) % parts), device_id_type=MESH
        )
        return carry

    lax.fori_loop(1, parts, greet, 0)

    def band(index):
        return pl.ds(pl.multiple_of(index * width, width), width)

    def scatter(source, target, send, recv, peer):
        return pltpu.make_async_remote_copy(
            src_ref=source,
            dst_ref=target,
            send_sem=send,
            recv_sem=recv,
            device_id=(peer, part),
            device_id_type=MESH,
        )

    def sum_copy(chunk, step, arriving=False):
        peer = partner(column, step, cols)
        slot = peer if arriving else column
        return scatter(
            outgoing_sum.at[chunk, band(peer)],
            incoming_sum.at[chunk, slot],
            sum_send.at[chunk, step - 1],
            sum_recv.at[chunk, slot],
            peer,
        )

    def self_copy(step, arriving=False):
        peer = partner(column, step, cols)
        slot = peer if arriving else column
        return scatter(
            outgoing_self.at[band(peer)],
            incoming_self.at[slot],
            self_send.at[step - 1],
            self_recv.at[slot],
            peer,
        )

    group = min(slots, 512)

    def choose(index, carry):
        start = pl.multiple_of(index * group, group)
        wanted = rows[:, pl.ds(start, group)]
        source = (
            lax.broadcasted_iota(jnp.int32, (parts, group), 1) + start
        ) // capacity == lax.broadcasted_iota(jnp.int32, (parts, group), 0)
        amount = dot(
            jnp.broadcast_to(count[...].astype(jnp.float32), (8, parts)).astype(jnp.bfloat16),
            source.astype(jnp.float32).astype(jnp.bfloat16),
            1,
            0,
        )[0:1, :]
        slot = (lax.broadcasted_iota(jnp.int32, (1, group), 1) % capacity).astype(jnp.float32)
        wanted = jnp.where(slot < amount, wanted, -1)
        hit = lax.broadcasted_iota(jnp.int32, (nodes, group), 0) == wanted
        pick[:, pl.ds(start, group)] = jnp.where(hit, 1.0, 0.0).astype(jnp.bfloat16)
        return carry

    lanes = slots // CHUNKS
    rate = parts // CHUNKS
    for load in loads[2:4]:
        load.wait()
    weights[...] = dot(neighw[...], proj[...], 0, 1).astype(jnp.bfloat16)
    for load in loads[:2]:
        load.wait()
    lax.fori_loop(0, slots // group, choose, 0)
    loads[4].wait()
    projected[...] = dot(weights[...], feat[...], 1, 0).astype(jnp.bfloat16)
    pl.semaphore_wait(barrier, cols + parts - 2)
    for chunk in range(CHUNKS):
        outgoing_sum[chunk] = dot(
            projected[...], pick[:, chunk * lanes : (chunk + 1) * lanes], 1, 0
        ).astype(jnp.bfloat16)
        for step in steps:
            sum_copy(chunk, step).start()
    for chunk in range(CHUNKS):
        own[chunk] = outgoing_sum[chunk, band(column), :]
    for load in loads[5:]:
        load.wait()
    weights_self[...] = dot(selfw[...], proj[...], 0, 1).astype(jnp.bfloat16)
    used = lax.broadcasted_iota(jnp.int32, (slot_count, nodes), 0) < degree[...]
    codes = jnp.where(used, neigh[...], -1)
    neigh[...] = codes
    depth = 256
    row_of = lax.broadcasted_iota(jnp.int32, (depth, LANES), 0).astype(jnp.float32).astype(jnp.bfloat16)
    one = jnp.ones((depth, LANES), jnp.bfloat16)
    zero = jnp.zeros((depth, LANES), jnp.bfloat16)

    def tally(index, carry):
        start = pl.multiple_of(index * depth, depth)
        for lane in range(nodes // LANES):
            there = slice(lane * LANES, (lane + 1) * LANES)
            near = jnp.clip(neigh[:, there] - start, -1, depth).astype(jnp.float32)
            total = zero
            for slot in range(slot_count):
                code = jnp.broadcast_to(near[slot : slot + 1, :], (16, LANES)).astype(jnp.bfloat16)
                code = jnp.concatenate([code] * (depth // 16), axis=0)
                total = total + jnp.where(row_of == code, one, zero)
            counts[pl.ds(start, depth), there] = total
        return carry

    lax.fori_loop(0, nodes // depth, tally, 0)
    share = 1.0 / degree[...].astype(jnp.float32)
    value = dot(projected[...], counts[0:nodes, :], 1, 0) * share
    value = value + dot(weights_self[...], feat[...], 1, 0)
    outgoing_self[...] = value.astype(jnp.bfloat16)
    for step in steps:
        self_copy(step).start()
    own_self[...] = outgoing_self[band(column), :].astype(jnp.float32)
    lax.fori_loop(nodes // depth, counts.shape[0] // depth, tally, 0)
    packed_in[part] = jnp.zeros((short, LANES), jnp.bfloat16)

    def part_copy(peer, slot):
        return pltpu.make_async_remote_copy(
            src_ref=packed_out.at[peer],
            dst_ref=packed_in.at[slot],
            send_sem=row_send.at[peer],
            recv_sem=row_recv.at[slot],
            device_id=(column, peer),
            device_id_type=MESH,
        )

    half = lax.broadcasted_iota(jnp.int32, (short, LANES), 1) // capacity

    for chunk in range(CHUNKS):
        for step in steps:
            sum_copy(chunk, step, True).wait_recv()
        total = own[chunk].astype(jnp.float32)
        for step in steps:
            total = total + incoming_sum[chunk, partner(column, step, cols)].astype(jnp.float32)
        first = chunk * rate
        for place in range(rate):
            block = total[:, place // fold * LANES : (place // fold + 1) * LANES]
            tight = None
            for piece in range(fold):
                shift = (piece - place % fold) * capacity % LANES
                value = block[piece * short : (piece + 1) * short, :]
                value = pltpu.roll(value, shift, 1) if shift else value
                tight = value if tight is None else jnp.where(half == piece, value, tight)
            packed_out[first + place] = tight.astype(jnp.bfloat16)
        for place in range(rate):

            @pl.when(first + place != part)
            def _():
                part_copy(first + place, part).start()

    remote[...] = jnp.zeros((width, nodes), jnp.float32)

    def gather(turn, carry):
        pair = (part // fold + turn) % pairs
        blocks = []
        for place in range(fold):
            peer = pair * fold + place

            @pl.when(peer != part)
            def _():
                part_copy(peer, peer).wait_recv()

        for place in range(fold):
            blocks.append(packed_in[pair * fold + place].astype(jnp.float32))
        pieces = []
        for piece in range(fold):
            value = jnp.zeros((short, LANES), jnp.float32)
            for place in range(fold):
                shift = (place - piece) * capacity % LANES
                block = pltpu.roll(blocks[place], shift, 1) if shift else blocks[place]
                value = jnp.where(half == place, block, value)
            pieces.append(value)
        table = jnp.concatenate(pieces, axis=0).astype(jnp.bfloat16)
        start = pl.multiple_of(nodes + pair * LANES, LANES)
        remote[...] += dot(table, counts[pl.ds(start, LANES), :], 1, 0)
        return carry

    lax.fori_loop(0, pairs, gather, 0)
    total = own_self[...]
    for step in steps:
        self_copy(step, True).wait_recv()
    for step in steps:
        total = total + incoming_self[partner(column, step, cols)].astype(jnp.float32)
    result = total + remote[...] * share
    out_ref[...] = jnp.maximum(result, 0.0).astype(out_ref.dtype)
    for step in steps:
        for chunk in range(CHUNKS):
            sum_copy(chunk, step).wait_send()
        self_copy(step).wait_send()

    def sent(peer, carry):
        @pl.when(peer != part)
        def _():
            part_copy(peer, part).wait_send()

        return carry

    lax.fori_loop(0, parts, sent, 0)


def local(features, proj_in, self_weight, neigh_weight, neighbors, degree, send_rows, send_count):
    cols = lax.axis_size("cols")
    parts = lax.axis_size("dom")
    inputs, hid = proj_in.shape
    width = hid // cols
    nodes = features.shape[1]
    slots = send_rows.shape[1]
    capacity = slots // parts
    fold = LANES // capacity
    short = width // fold
    degree = degree.reshape(1, nodes)
    arguments = (
        features,
        proj_in,
        self_weight,
        neigh_weight,
        neighbors,
        degree,
        send_rows,
        send_count,
    )
    bf16 = jnp.bfloat16
    copies = pltpu.SemaphoreType.DMA
    limit = (16 << 20) + (slots * nodes + slots * hid + hid * nodes * 8) * 4
    return pl.pallas_call(
        functools.partial(kernel, cols, parts, capacity),
        out_shape=jax.ShapeDtypeStruct((width, nodes), bf16),
        in_specs=[pl.BlockSpec(memory_space=pltpu.HBM)] * len(arguments),
        out_specs=pl.BlockSpec(memory_space=pltpu.VMEM),
        scratch_shapes=[pltpu.VMEM(a.shape, a.dtype) for a in arguments]
        + [
            pltpu.VMEM((hid, inputs), bf16),
            pltpu.VMEM((hid, inputs), bf16),
            pltpu.VMEM((hid, nodes), bf16),
            pltpu.VMEM((CHUNKS, width, slots // CHUNKS), bf16),
            pltpu.VMEM((width, nodes), jnp.float32),
            pltpu.VMEM((CHUNKS, hid, slots // CHUNKS), bf16),
            pltpu.VMEM((hid, nodes), bf16),
            pltpu.VMEM((CHUNKS, cols, width, slots // CHUNKS), bf16),
            pltpu.VMEM((cols, width, nodes), bf16),
            pltpu.VMEM((nodes, slots), bf16),
            pltpu.VMEM((parts, short, LANES), bf16),
            pltpu.VMEM((parts, short, LANES), bf16),
            pltpu.VMEM((width, nodes), jnp.float32),
            pltpu.VMEM((nodes + slots, nodes), bf16),
            copies((len(arguments),)),
            copies((CHUNKS, cols - 1)),
            copies((CHUNKS, cols)),
            copies((parts,)),
            copies((parts,)),
            copies((cols - 1,)),
            copies((cols,)),
        ],
        compiler_params=pltpu.CompilerParams(
            collective_id=0, has_side_effects=True, vmem_limit_bytes=limit
        ),
        name="layer",
    )(*[pltpu.with_memory_space_constraint(a, pltpu.HBM) for a in arguments])


def solution(mesh):
    return jax.shard_map(
        local,
        mesh=mesh,
        in_specs=(
            P("cols", "dom"),
            P("cols", None),
            P(),
            P(),
            P(None, "dom"),
            P("dom"),
            P("dom", None),
            P("dom", None),
        ),
        out_specs=P("cols", "dom"),
        check_vma=False,
    )
```

time: 22.3 us -> 15 us (0.67)
  Pallas kernels: 20.6 us -> 14.2 us
  local copies, waits for them, and re-layouts: 1.47 us -> 0.63 us
    pallas_call x1, Pallas kernels: 20.6 us -> 14.2 us  [local(): pl.pallas_call(functools.partial(kernel, cols, parts, capacity), out_shap...]
    unnamed x1, local copies, waits for them, and re-layouts: 1.47 us -> 0.63 us
where the time goes in v3:
time: 15 us; the launch traced here: 14.9 us
  Pallas kernels  14.2 us (95%)
  local copies, waits for them, and re-layouts  0.63 us (4%)
    pallas_call x1, Pallas kernels, local(): pl.pallas_call(functools.partial(kernel, cols, parts, capacity), out_shap...  14.2 us
    unnamed x1, local copies, waits for them, and re-layouts  0.63 us

profile of v3, /device:TPU:0, one launch (start us, length us, event | category | flops | bytes accessed | tf_op | source)
XLA Modules:
  0.0 14.9 jit_solution(15446608594717994583)
XLA Ops:
  0.0 14.2 %layer.1 = bf16[64,512]{1,0:T(8,128)(2,1)S(1)} custom-call(bf16[192,512]{1,0:T(8,128)(2,1)} %feat_hbm.1, bf16[192,256]{1,0:T(8,128)(2,1)} %proj_hbm.1, bf16[256,256]{1,0:T(8,128)(2,1)} %selfw_hbm.1, bf16[256,256]{1,0:T(8,128)(2,1)} %neighw_hbm.1, s32[16,512]{1,0:T(8,128)} %neigh_hbm.1, s32[1,512]{1,0:T(1,128)} %bitcast.1, s32[1,512]{1,0:T(1,128)} %rows_hbm.1, ...), custom_call_target="tpu_custom_call" | custom-call | tf_op jit(solution)/shard_map/layer/pallas_call | solution.py:335
  14.2 0.6 %copy.10 = bf16[64,512]{1,0:T(8,128)(2,1)} copy(bf16[64,512]{1,0:T(8,128)(2,1)S(1)} %layer.1) | data formatting | bytes 131072

commit v4 on v3

--- a/solution.py
+++ b/solution.py
@@ -10,6 +10,7 @@
 MESH = pl.DeviceIdType.MESH
 LANES = 128
 CHUNKS = 4
+NEAR = 2
 
 
 def dot(left, right, left_dim, right_dim):
@@ -71,6 +72,7 @@
     row_recv,
     self_send,
     self_recv,
+    known,
 ):
     column = lax.axis_index("cols")
     part = lax.axis_index("dom")
@@ -83,15 +85,57 @@
     pairs = parts // fold
     steps = sorted(range(1, cols), key=lambda step: -bin(step).count("1"))
 
+    barrier = pltpu.get_barrier_semaphore()
+    for step in range(1, cols):
+        pl.semaphore_signal(
+            barrier, inc=1, device_id=((column + step) % cols, part), device_id_type=MESH
+        )
+
+    def aside(distance, act):
+        for way, offset in enumerate((-distance, distance)):
+
+            @pl.when((part + offset >= 0) & (part + offset < parts))
+            def _():
+                act(way, part + offset)
+
+    for distance in range(1, NEAR + 1):
+        aside(
+            distance,
+            lambda way, peer: pl.semaphore_signal(
+                barrier, inc=1, device_id=(column, peer), device_id_type=MESH
+            ),
+        )
+
+    def enter():
+        peers = cols - 1
+        for distance in range(1, NEAR + 1):
+            peers = peers + (part - distance + parts) // parts + 1 - (part + distance) // parts
+        pl.semaphore_wait(barrier, peers)
+
+    def tell(stage):
+        aside(
+            NEAR << stage,
+            lambda way, peer: pl.semaphore_signal(
+                known.at[stage, 1 - way], inc=1, device_id=(column, peer), device_id_type=MESH
+            ),
+        )
+
+    def hear(stage):
+        aside(NEAR << stage, lambda way, peer: pl.semaphore_wait(known.at[stage, way], 1))
+
+    stages = 0
+    while NEAR << stages < parts - 1:
+        stages += 1
+
     loads = [
         pltpu.make_async_copy(source, target, in_sem.at[i])
         for i, (source, target) in enumerate(
             (
                 (rows_hbm, rows),
                 (count_hbm, count),
+                (feat_hbm, feat),
                 (neighw_hbm, neighw),
                 (proj_hbm, proj),
-                (feat_hbm, feat),
                 (selfw_hbm, selfw),
                 (neigh_hbm, neigh),
                 (degree_hbm, degree),
@@ -100,20 +144,6 @@
     ]
     for load in loads:
         load.start()
-
-    barrier = pltpu.get_barrier_semaphore()
-    for step in range(1, cols):
-        pl.semaphore_signal(
-            barrier, inc=1, device_id=((column + step) % cols, part), device_id_type=MESH
-        )
-
-    def greet(step, carry):
-        pl.semaphore_signal(
-            barrier, inc=1, device_id=(column, (part + step) % parts), device_id_type=MESH
-        )
-        return carry
-
-    lax.fori_loop(1, parts, greet, 0)
 
     def band(index):
         return pl.ds(pl.multiple_of(index * width, width), width)
@@ -150,43 +180,43 @@
             peer,
         )
 
-    group = min(slots, 512)
-
-    def choose(index, carry):
-        start = pl.multiple_of(index * group, group)
-        wanted = rows[:, pl.ds(start, group)]
-        source = (
-            lax.broadcasted_iota(jnp.int32, (parts, group), 1) + start
-        ) // capacity == lax.broadcasted_iota(jnp.int32, (parts, group), 0)
-        amount = dot(
-            jnp.broadcast_to(count[...].astype(jnp.float32), (8, parts)).astype(jnp.bfloat16),
-            source.astype(jnp.float32).astype(jnp.bfloat16),
-            1,
-            0,
-        )[0:1, :]
-        slot = (lax.broadcasted_iota(jnp.int32, (1, group), 1) % capacity).astype(jnp.float32)
-        wanted = jnp.where(slot < amount, wanted, -1)
-        hit = lax.broadcasted_iota(jnp.int32, (nodes, group), 0) == wanted
-        pick[:, pl.ds(start, group)] = jnp.where(hit, 1.0, 0.0).astype(jnp.bfloat16)
-        return carry
-
     lanes = slots // CHUNKS
     rate = parts // CHUNKS
-    for load in loads[2:4]:
+    group = min(lanes, 512)
+
+    def choose(chunk):
+        amount = jnp.zeros((1, lanes), jnp.int32)
+        place = lax.broadcasted_iota(jnp.int32, (1, lanes), 1)
+        for index in range(rate):
+            here = place // capacity == index
+            peer = chunk * rate + index
+            amount = jnp.where(here, count[:, peer : peer + 1], amount)
+        wanted = jnp.where(
+            place % capacity < amount, rows[:, chunk * lanes : (chunk + 1) * lanes], -1
+        )
+        for start in range(0, lanes, group):
+            hit = (
+                lax.broadcasted_iota(jnp.int32, (nodes, group), 0)
+                == wanted[:, start : start + group]
+            )
+            there = slice(chunk * lanes + start, chunk * lanes + start + group)
+            pick[:, there] = jnp.where(hit, 1.0, 0.0).astype(jnp.bfloat16)
+
+    for load in loads[:5]:
         load.wait()
-    weights[...] = dot(neighw[...], proj[...], 0, 1).astype(jnp.bfloat16)
-    for load in loads[:2]:
-        load.wait()
-    lax.fori_loop(0, slots // group, choose, 0)
-    loads[4].wait()
-    projected[...] = dot(weights[...], feat[...], 1, 0).astype(jnp.bfloat16)
-    pl.semaphore_wait(barrier, cols + parts - 2)
+    turned = dot(neighw[...], proj[...], 0, 1).astype(jnp.bfloat16)
     for chunk in range(CHUNKS):
-        outgoing_sum[chunk] = dot(
-            projected[...], pick[:, chunk * lanes : (chunk + 1) * lanes], 1, 0
-        ).astype(jnp.bfloat16)
+        choose(chunk)
+    value = dot(turned, feat[...], 1, 0).astype(jnp.bfloat16)
+    projected[...] = value
+    whole = dot(value, pick[...], 1, 0).astype(jnp.bfloat16)
+    for chunk in range(CHUNKS):
+        outgoing_sum[chunk] = whole[:, chunk * lanes : (chunk + 1) * lanes]
+    enter()
+    for chunk in range(CHUNKS):
         for step in steps:
             sum_copy(chunk, step).start()
+    tell(0)
     for chunk in range(CHUNKS):
         own[chunk] = outgoing_sum[chunk, band(column), :]
     for load in loads[5:]:
@@ -221,6 +251,10 @@
     for step in steps:
         self_copy(step).start()
     own_self[...] = outgoing_self[band(column), :].astype(jnp.float32)
+    if stages:
+        hear(0)
+    if stages > 1:
+        tell(1)
     lax.fori_loop(nodes // depth, counts.shape[0] // depth, tally, 0)
     packed_in[part] = jnp.zeros((short, LANES), jnp.bfloat16)
 
@@ -236,6 +270,10 @@
 
     half = lax.broadcasted_iota(jnp.int32, (short, LANES), 1) // capacity
 
+    for stage in range(1, stages):
+        hear(stage)
+        if stage + 1 < stages:
+            tell(stage + 1)
     for chunk in range(CHUNKS):
         for step in steps:
             sum_copy(chunk, step, True).wait_recv()
@@ -360,6 +398,7 @@
             copies((parts,)),
             copies((cols - 1,)),
             copies((cols,)),
+            pltpu.SemaphoreType.REGULAR((parts.bit_length(), 2)),
         ],
         compiler_params=pltpu.CompilerParams(
             collective_id=0, has_side_effects=True, vmem_limit_bytes=limit

time: 15 us -> 14.5 us (0.967)
  Pallas kernels: 14.2 us -> 13.7 us
    pallas_call x1, Pallas kernels: 14.2 us -> 13.7 us  [local(): pl.pallas_call(functools.partial(kernel, cols, parts, capacity), out_shap...]
where the time goes in v4:
time: 14.5 us; the launch traced here: 14.4 us
  Pallas kernels  13.7 us (94%)
  local copies, waits for them, and re-layouts  0.63 us (4%)
    pallas_call x1, Pallas kernels, local(): pl.pallas_call(functools.partial(kernel, cols, parts, capacity), out_shap...  13.7 us
    unnamed x1, local copies, waits for them, and re-layouts  0.63 us

profile of v4, /device:TPU:0, one launch (start us, length us, event | category | flops | bytes accessed | tf_op | source)
XLA Modules:
  0.0 14.4 jit_solution(18417383046201311004)
XLA Ops:
  0.0 13.7 %layer.1 = bf16[64,512]{1,0:T(8,128)(2,1)S(1)} custom-call(bf16[192,512]{1,0:T(8,128)(2,1)} %feat_hbm.1, bf16[192,256]{1,0:T(8,128)(2,1)} %proj_hbm.1, bf16[256,256]{1,0:T(8,128)(2,1)} %selfw_hbm.1, bf16[256,256]{1,0:T(8,128)(2,1)} %neighw_hbm.1, s32[16,512]{1,0:T(8,128)} %neigh_hbm.1, s32[1,512]{1,0:T(1,128)} %bitcast.1, s32[1,512]{1,0:T(1,128)} %rows_hbm.1, ...), custom_call_target="tpu_custom_call" | custom-call | tf_op jit(solution)/shard_map/layer/pallas_call | solution.py:373
  13.7 0.6 %copy.10 = bf16[64,512]{1,0:T(8,128)(2,1)} copy(bf16[64,512]{1,0:T(8,128)(2,1)S(1)} %layer.1) | data formatting | bytes 131072

commit v5 on v4

--- a/solution.py
+++ b/solution.py
@@ -10,7 +10,6 @@
 MESH = pl.DeviceIdType.MESH
 LANES = 128
 CHUNKS = 4
-NEAR = 2
 
 
 def dot(left, right, left_dim, right_dim):
@@ -54,7 +53,6 @@
     weights,
     weights_self,
     projected,
-    own,
     own_self,
     outgoing_sum,
     outgoing_self,
@@ -81,51 +79,11 @@
     slots = rows.shape[1]
     slot_count = neigh.shape[0]
     fold = LANES // capacity
-    short = width // fold
     pairs = parts // fold
+    pair = part // fold
+    member = part % fold
+    carrier = pair * fold + fold - 1
     steps = sorted(range(1, cols), key=lambda step: -bin(step).count("1"))
-
-    barrier = pltpu.get_barrier_semaphore()
-    for step in range(1, cols):
-        pl.semaphore_signal(
-            barrier, inc=1, device_id=((column + step) % cols, part), device_id_type=MESH
-        )
-
-    def aside(distance, act):
-        for way, offset in enumerate((-distance, distance)):
-
-            @pl.when((part + offset >= 0) & (part + offset < parts))
-            def _():
-                act(way, part + offset)
-
-    for distance in range(1, NEAR + 1):
-        aside(
-            distance,
-            lambda way, peer: pl.semaphore_signal(
-                barrier, inc=1, device_id=(column, peer), device_id_type=MESH
-            ),
-        )
-
-    def enter():
-        peers = cols - 1
-        for distance in range(1, NEAR + 1):
-            peers = peers + (part - distance + parts) // parts + 1 - (part + distance) // parts
-        pl.semaphore_wait(barrier, peers)
-
-    def tell(stage):
-        aside(
-            NEAR << stage,
-            lambda way, peer: pl.semaphore_signal(
-                known.at[stage, 1 - way], inc=1, device_id=(column, peer), device_id_type=MESH
-            ),
-        )
-
-    def hear(stage):
-        aside(NEAR << stage, lambda way, peer: pl.semaphore_wait(known.at[stage, way], 1))
-
-    stages = 0
-    while NEAR << stages < parts - 1:
-        stages += 1
 
     loads = [
         pltpu.make_async_copy(source, target, in_sem.at[i])
@@ -142,32 +100,88 @@
             )
         )
     ]
-    for load in loads:
+    for load in loads[:5]:
+        load.start()
+
+    barrier = pltpu.get_barrier_semaphore()
+
+    def greet(target, place):
+        pl.semaphore_signal(
+            barrier, inc=1, device_id=(target, place), device_id_type=MESH
+        )
+
+    for step in range(cols):
+        for turn in range(1 if step == 0 else 0, fold):
+            greet((column + step) % cols, pair * fold + (part + turn) % fold)
+    for way in (-1, 1):
+
+        @pl.when((pair + way >= 0) & (pair + way < pairs))
+        def _():
+            for place in range(fold):
+                greet(column, (pair + way) * fold + place)
+
+    def enter():
+        beside = (pair - 1 + pairs) // pairs + 1 - (pair + 1) // pairs
+        pl.semaphore_wait(barrier, cols * fold - 1 + beside * fold)
+
+    def aside(distance, act):
+        for way, offset in enumerate((-distance, distance)):
+
+            @pl.when((part + offset >= 0) & (part + offset < parts))
+            def _():
+                act(way, part + offset)
+
+    def tell(stage):
+        aside(
+            fold << stage,
+            lambda way, peer: pl.semaphore_signal(
+                known.at[stage, 1 - way], inc=1, device_id=(column, peer), device_id_type=MESH
+            ),
+        )
+
+    def hear(stage):
+        aside(fold << stage, lambda way, peer: pl.semaphore_wait(known.at[stage, way], 1))
+
+    stages = 0
+    while 1 << stages < pairs - 1:
+        stages += 1
+
+    for load in loads[5:]:
         load.start()
 
     def band(index):
         return pl.ds(pl.multiple_of(index * width, width), width)
 
-    def scatter(source, target, send, recv, peer):
+    def scatter(source, target, send, recv, peer, place):
         return pltpu.make_async_remote_copy(
             src_ref=source,
             dst_ref=target,
             send_sem=send,
             recv_sem=recv,
-            device_id=(peer, part),
+            device_id=(peer, place),
             device_id_type=MESH,
         )
 
-    def sum_copy(chunk, step, arriving=False):
+    def sum_copy(chunk, step, place=None):
         peer = partner(column, step, cols)
-        slot = peer if arriving else column
+        slot = column if place is None else peer
+        place = member if place is None else place
         return scatter(
             outgoing_sum.at[chunk, band(peer)],
-            incoming_sum.at[chunk, slot],
-            sum_send.at[chunk, step - 1],
-            sum_recv.at[chunk, slot],
+            incoming_sum.at[chunk, place, slot],
+            sum_send.at[chunk, step],
+            sum_recv.at[chunk, place, slot],
             peer,
-        )
+            carrier,
+        )
+
+    def sum_start(chunk):
+        for step in steps:
+            sum_copy(chunk, step).start()
+
+        @pl.when(part != carrier)
+        def _():
+            sum_copy(chunk, 0).start()
 
     def self_copy(step, arriving=False):
         peer = partner(column, step, cols)
@@ -178,6 +192,7 @@
             self_send.at[step - 1],
             self_recv.at[slot],
             peer,
+            part,
         )
 
     lanes = slots // CHUNKS
@@ -204,21 +219,23 @@
 
     for load in loads[:5]:
         load.wait()
+    choose(0)
+    picked = dot(feat[...], pick[:, 0:lanes], 1, 0).astype(jnp.bfloat16)
     turned = dot(neighw[...], proj[...], 0, 1).astype(jnp.bfloat16)
-    for chunk in range(CHUNKS):
+    weights[...] = turned
+    outgoing_sum[0] = dot(turned, picked, 1, 0).astype(jnp.bfloat16)
+    enter()
+    sum_start(0)
+    tell(0)
+    for chunk in range(1, CHUNKS):
         choose(chunk)
-    value = dot(turned, feat[...], 1, 0).astype(jnp.bfloat16)
+    value = dot(weights[...], feat[...], 1, 0).astype(jnp.bfloat16)
     projected[...] = value
-    whole = dot(value, pick[...], 1, 0).astype(jnp.bfloat16)
-    for chunk in range(CHUNKS):
-        outgoing_sum[chunk] = whole[:, chunk * lanes : (chunk + 1) * lanes]
-    enter()
-    for chunk in range(CHUNKS):
-        for step in steps:
-            sum_copy(chunk, step).start()
-    tell(0)
-    for chunk in range(CHUNKS):
-        own[chunk] = outgoing_sum[chunk, band(column), :]
+    whole = dot(value, pick[:, lanes:], 1, 0).astype(jnp.bfloat16)
+    for chunk in range(1, CHUNKS):
+        outgoing_sum[chunk] = whole[:, (chunk - 1) * lanes : chunk * lanes]
+    for chunk in range(1, CHUNKS):
+        sum_start(chunk)
     for load in loads[5:]:
         load.wait()
     weights_self[...] = dot(selfw[...], proj[...], 0, 1).astype(jnp.bfloat16)
@@ -256,7 +273,6 @@
     if stages > 1:
         tell(1)
     lax.fori_loop(nodes // depth, counts.shape[0] // depth, tally, 0)
-    packed_in[part] = jnp.zeros((short, LANES), jnp.bfloat16)
 
     def part_copy(peer, slot):
         return pltpu.make_async_remote_copy(
@@ -268,82 +284,89 @@
             device_id_type=MESH,
         )
 
-    half = lax.broadcasted_iota(jnp.int32, (short, LANES), 1) // capacity
+    half = lax.broadcasted_iota(jnp.int32, (width, LANES), 1) // capacity
 
     for stage in range(1, stages):
         hear(stage)
         if stage + 1 < stages:
             tell(stage + 1)
-    for chunk in range(CHUNKS):
-        for step in steps:
-            sum_copy(chunk, step, True).wait_recv()
-        total = own[chunk].astype(jnp.float32)
-        for step in steps:
-            total = total + incoming_sum[chunk, partner(column, step, cols)].astype(jnp.float32)
-        first = chunk * rate
-        for place in range(rate):
-            block = total[:, place // fold * LANES : (place // fold + 1) * LANES]
-            tight = None
-            for piece in range(fold):
-                shift = (piece - place % fold) * capacity % LANES
-                value = block[piece * short : (piece + 1) * short, :]
-                value = pltpu.roll(value, shift, 1) if shift else value
-                tight = value if tight is None else jnp.where(half == piece, value, tight)
-            packed_out[first + place] = tight.astype(jnp.bfloat16)
-        for place in range(rate):
-
-            @pl.when(first + place != part)
-            def _():
-                part_copy(first + place, part).start()
+
+    @pl.when(part == carrier)
+    def _():
+        for chunk in range(CHUNKS):
+            totals = []
+            for place in range(fold):
+                for step in steps:
+                    sum_copy(chunk, step, place).wait_recv()
+                if place == fold - 1:
+                    total = outgoing_sum[chunk, band(column), :].astype(jnp.float32)
+                else:
+                    sum_copy(chunk, 0, place).wait_recv()
+                    total = incoming_sum[chunk, place, column].astype(jnp.float32)
+                for step in steps:
+                    value = incoming_sum[chunk, place, partner(column, step, cols)]
+                    total = total + value.astype(jnp.float32)
+                totals.append(total)
+            first = chunk * rate
+            for target in range(rate):
+                there = slice(target // fold * LANES, (target // fold + 1) * LANES)
+                tight = None
+                for place in range(fold):
+                    shift = (place - target % fold) * capacity % LANES
+                    value = totals[place][:, there]
+                    value = pltpu.roll(value, shift, 1) if shift else value
+                    tight = value if tight is None else jnp.where(half == place, value, tight)
+                packed_out[first + target] = tight.astype(jnp.bfloat16)
+            for target in range(rate):
+
+                @pl.when(first + target != part)
+                def _():
+                    part_copy(first + target, pair).start()
+
+        packed_in[pair] = packed_out[part]
 
     remote[...] = jnp.zeros((width, nodes), jnp.float32)
 
     def gather(turn, carry):
-        pair = (part // fold + turn) % pairs
-        blocks = []
-        for place in range(fold):
-            peer = pair * fold + place
-
-            @pl.when(peer != part)
-            def _():
-                part_copy(peer, peer).wait_recv()
-
-        for place in range(fold):
-            blocks.append(packed_in[pair * fold + place].astype(jnp.float32))
-        pieces = []
-        for piece in range(fold):
-            value = jnp.zeros((short, LANES), jnp.float32)
-            for place in range(fold):
-                shift = (place - piece) * capacity % LANES
-                block = pltpu.roll(blocks[place], shift, 1) if shift else blocks[place]
-                value = jnp.where(half == place, block, value)
-            pieces.append(value)
-        table = jnp.concatenate(pieces, axis=0).astype(jnp.bfloat16)
-        start = pl.multiple_of(nodes + pair * LANES, LANES)
-        remote[...] += dot(table, counts[pl.ds(start, LANES), :], 1, 0)
+        source = (pair + turn) % pairs
+
+        @pl.when(source * fold + fold - 1 != part)
+        def _():
+            part_copy(part, source).wait_recv()
+
+        start = pl.multiple_of(nodes + source * LANES, LANES)
+        remote[...] += dot(packed_in[source], counts[pl.ds(start, LANES), :], 1, 0)
         return carry
 
-    lax.fori_loop(0, pairs, gather, 0)
+    for step in steps:
+        for chunk in range(CHUNKS):
+            sum_copy(chunk, step).wait_send()
+        self_copy(step).wait_send()
+
+    @pl.when(part != carrier)
+    def _():
+        for chunk in range(CHUNKS):
+            sum_copy(chunk, 0).wait_send()
+
+    lax.fori_loop(0, pairs - 1, gather, 0)
     total = own_self[...]
     for step in steps:
         self_copy(step, True).wait_recv()
     for step in steps:
         total = total + incoming_self[partner(column, step, cols)].astype(jnp.float32)
-    result = total + remote[...] * share
+    own_self[...] = total
+
+    def sent(peer, carry):
+        @pl.when((part == carrier) & (peer != part))
+        def _():
+            part_copy(peer, pair).wait_send()
+
+        return carry
+
+    lax.fori_loop(0, parts, sent, 0)
+    gather(pairs - 1, 0)
+    result = own_self[...] + remote[...] * share
     out_ref[...] = jnp.maximum(result, 0.0).astype(out_ref.dtype)
-    for step in steps:
-        for chunk in range(CHUNKS):
-            sum_copy(chunk, step).wait_send()
-        self_copy(step).wait_send()
-
-    def sent(peer, carry):
-        @pl.when(peer != part)
-        def _():
-            part_copy(peer, part).wait_send()
-
-        return carry
-
-    lax.fori_loop(0, parts, sent, 0)
 
 
 def local(features, proj_in, self_weight, neigh_weight, neighbors, degree, send_rows, send_count):
@@ -355,7 +378,6 @@
     slots = send_rows.shape[1]
     capacity = slots // parts
     fold = LANES // capacity
-    short = width // fold
     degree = degree.reshape(1, nodes)
     arguments = (
         features,
@@ -380,22 +402,21 @@
             pltpu.VMEM((hid, inputs), bf16),
             pltpu.VMEM((hid, inputs), bf16),
             pltpu.VMEM((hid, nodes), bf16),
-            pltpu.VMEM((CHUNKS, width, slots // CHUNKS), bf16),
             pltpu.VMEM((width, nodes), jnp.float32),
             pltpu.VMEM((CHUNKS, hid, slots // CHUNKS), bf16),
             pltpu.VMEM((hid, nodes), bf16),
-            pltpu.VMEM((CHUNKS, cols, width, slots // CHUNKS), bf16),
+            pltpu.VMEM((CHUNKS, fold, cols, width, slots // CHUNKS), bf16),
             pltpu.VMEM((cols, width, nodes), bf16),
             pltpu.VMEM((nodes, slots), bf16),
-            pltpu.VMEM((parts, short, LANES), bf16),
-            pltpu.VMEM((parts, short, LANES), bf16),
+            pltpu.VMEM((parts, width, LANES), bf16),
+            pltpu.VMEM((parts // fold, width, LANES), bf16),
             pltpu.VMEM((width, nodes), jnp.float32),
             pltpu.VMEM((nodes + slots, nodes), bf16),
             copies((len(arguments),)),
-            copies((CHUNKS, cols - 1)),
             copies((CHUNKS, cols)),
+            copies((CHUNKS, fold, cols)),
             copies((parts,)),
-            copies((parts,)),
+            copies((parts // fold,)),
             copies((cols - 1,)),
             copies((cols,)),
             pltpu.SemaphoreType.REGULAR((parts.bit_length(), 2)),

time: 14.5 us -> 13.7 us (0.945)
  Pallas kernels: 13.7 us -> 12.9 us
    pallas_call x1, Pallas kernels: 13.7 us -> 12.9 us  [local(): pl.pallas_call(functools.partial(kernel, cols, parts, capacity), out_shap...]
where the time goes in v5:
time: 13.7 us; the launch traced here: 13.5 us
  Pallas kernels  12.9 us (94%)
  local copies, waits for them, and re-layouts  0.63 us (5%)
    pallas_call x1, Pallas kernels, local(): pl.pallas_call(functools.partial(kernel, cols, parts, capacity), out_shap...  12.9 us
    unnamed x1, local copies, waits for them, and re-layouts  0.63 us

profile of v5, /device:TPU:0, one launch (start us, length us, event | category | flops | bytes accessed | tf_op | source)
XLA Modules:
  0.0 13.5 jit_solution(18432296034404666436)
XLA Ops:
  0.0 12.9 %layer.1 = bf16[64,512]{1,0:T(8,128)(2,1)S(1)} custom-call(bf16[192,512]{1,0:T(8,128)(2,1)} %feat_hbm.1, bf16[192,256]{1,0:T(8,128)(2,1)} %proj_hbm.1, bf16[256,256]{1,0:T(8,128)(2,1)} %selfw_hbm.1, bf16[256,256]{1,0:T(8,128)(2,1)} %neighw_hbm.1, s32[16,512]{1,0:T(8,128)} %neigh_hbm.1, s32[1,512]{1,0:T(1,128)} %bitcast.1, s32[1,512]{1,0:T(1,128)} %rows_hbm.1, ...), custom_call_target="tpu_custom_call" | custom-call | tf_op jit(solution)/shard_map/layer/pallas_call | solution.py:395
  12.9 0.6 %copy.10 = bf16[64,512]{1,0:T(8,128)(2,1)} copy(bf16[64,512]{1,0:T(8,128)(2,1)S(1)} %layer.1) | data formatting | bytes 131072

commit v6 on v5

--- a/solution.py
+++ b/solution.py
@@ -27,6 +27,13 @@
             size = 1 << bit
             other = other + size - 2 * size * (me // size % 2)
     return other
+
+
+def rounds(pairs):
+    stages = 0
+    while 1 << stages < pairs - 1:
+        stages += 1
+    return stages
 
 
 def kernel(
@@ -64,11 +71,9 @@
     remote,
     counts,
     in_sem,
-    sum_send,
+    sends,
     sum_recv,
-    row_send,
     row_recv,
-    self_send,
     self_recv,
     known,
 ):
@@ -142,9 +147,7 @@
     def hear(stage):
         aside(fold << stage, lambda way, peer: pl.semaphore_wait(known.at[stage, way], 1))
 
-    stages = 0
-    while 1 << stages < pairs - 1:
-        stages += 1
+    stages = rounds(pairs)
 
     for load in loads[5:]:
         load.start()
@@ -162,18 +165,19 @@
             device_id_type=MESH,
         )
 
-    def sum_copy(chunk, step, place=None):
+    def sum_copy(chunk, step):
         peer = partner(column, step, cols)
-        slot = column if place is None else peer
-        place = member if place is None else place
         return scatter(
             outgoing_sum.at[chunk, band(peer)],
-            incoming_sum.at[chunk, place, slot],
-            sum_send.at[chunk, step],
-            sum_recv.at[chunk, place, slot],
+            incoming_sum.at[chunk, member * cols + column],
+            sends.at[0],
+            sum_recv.at[chunk],
             peer,
             carrier,
         )
+
+    def settle(refs, semaphore):
+        pltpu.make_async_copy(refs, refs, semaphore).wait()
 
     def sum_start(chunk):
         for step in steps:
@@ -183,14 +187,13 @@
         def _():
             sum_copy(chunk, 0).start()
 
-    def self_copy(step, arriving=False):
+    def self_copy(step):
         peer = partner(column, step, cols)
-        slot = peer if arriving else column
         return scatter(
             outgoing_self.at[band(peer)],
-            incoming_self.at[slot],
-            self_send.at[step - 1],
-            self_recv.at[slot],
+            incoming_self.at[column],
+            sends.at[1],
+            self_recv.at[0],
             peer,
             part,
         )
@@ -278,7 +281,7 @@
         return pltpu.make_async_remote_copy(
             src_ref=packed_out.at[peer],
             dst_ref=packed_in.at[slot],
-            send_sem=row_send.at[peer],
+            send_sem=sends.at[2],
             recv_sem=row_recv.at[slot],
             device_id=(column, peer),
             device_id_type=MESH,
@@ -294,17 +297,15 @@
     @pl.when(part == carrier)
     def _():
         for chunk in range(CHUNKS):
+            settle(incoming_sum.at[chunk, pl.ds(0, fold * cols - 1)], sum_recv.at[chunk])
             totals = []
             for place in range(fold):
-                for step in steps:
-                    sum_copy(chunk, step, place).wait_recv()
                 if place == fold - 1:
                     total = outgoing_sum[chunk, band(column), :].astype(jnp.float32)
                 else:
-                    sum_copy(chunk, 0, place).wait_recv()
-                    total = incoming_sum[chunk, place, column].astype(jnp.float32)
+                    total = incoming_sum[chunk, place * cols + column].astype(jnp.float32)
                 for step in steps:
-                    value = incoming_sum[chunk, place, partner(column, step, cols)]
+                    value = incoming_sum[chunk, place * cols + partner(column, step, cols)]
                     total = total + value.astype(jnp.float32)
                 totals.append(total)
             first = chunk * rate
@@ -338,32 +339,24 @@
         remote[...] += dot(packed_in[source], counts[pl.ds(start, LANES), :], 1, 0)
         return carry
 
-    for step in steps:
-        for chunk in range(CHUNKS):
-            sum_copy(chunk, step).wait_send()
-        self_copy(step).wait_send()
-
-    @pl.when(part != carrier)
-    def _():
-        for chunk in range(CHUNKS):
-            sum_copy(chunk, 0).wait_send()
-
     lax.fori_loop(0, pairs - 1, gather, 0)
     total = own_self[...]
-    for step in steps:
-        self_copy(step, True).wait_recv()
+    settle(incoming_self.at[pl.ds(0, cols - 1)], self_recv.at[0])
     for step in steps:
         total = total + incoming_self[partner(column, step, cols)].astype(jnp.float32)
     own_self[...] = total
 
-    def sent(peer, carry):
-        @pl.when((part == carrier) & (peer != part))
-        def _():
-            part_copy(peer, pair).wait_send()
-
-        return carry
-
-    lax.fori_loop(0, parts, sent, 0)
+    settle(outgoing_self.at[pl.ds(0, (cols - 1) * width)], sends.at[1])
+
+    @pl.when(part == carrier)
+    def _():
+        settle(outgoing_sum.at[:, pl.ds(0, (cols - 1) * width)], sends.at[0])
+        settle(packed_out.at[pl.ds(0, parts - 1)], sends.at[2])
+
+    @pl.when(part != carrier)
+    def _():
+        settle(outgoing_sum, sends.at[0])
+
     gather(pairs - 1, 0)
     result = own_self[...] + remote[...] * share
     out_ref[...] = jnp.maximum(result, 0.0).astype(out_ref.dtype)
@@ -405,7 +398,7 @@
             pltpu.VMEM((width, nodes), jnp.float32),
             pltpu.VMEM((CHUNKS, hid, slots // CHUNKS), bf16),
             pltpu.VMEM((hid, nodes), bf16),
-            pltpu.VMEM((CHUNKS, fold, cols, width, slots // CHUNKS), bf16),
+            pltpu.VMEM((CHUNKS, fold * cols, width, slots // CHUNKS), bf16),
             pltpu.VMEM((cols, width, nodes), bf16),
             pltpu.VMEM((nodes, slots), bf16),
             pltpu.VMEM((parts, width, LANES), bf16),
@@ -413,13 +406,11 @@
             pltpu.VMEM((width, nodes), jnp.float32),
             pltpu.VMEM((nodes + slots, nodes), bf16),
             copies((len(arguments),)),
-            copies((CHUNKS, cols)),
-            copies((CHUNKS, fold, cols)),
-            copies((parts,)),
+            copies((3,)),
+            copies((CHUNKS,)),
             copies((parts // fold,)),
-            copies((cols - 1,)),
-            copies((cols,)),
-            pltpu.SemaphoreType.REGULAR((parts.bit_length(), 2)),
+            copies((1,)),
+            pltpu.SemaphoreType.REGULAR((max(1, rounds(parts // fold)), 2)),
         ],
         compiler_params=pltpu.CompilerParams(
             collective_id=0, has_side_effects=True, vmem_limit_bytes=limit

time: 13.7 us -> 13.2 us (0.964)
  Pallas kernels: 12.9 us -> 12.4 us
    pallas_call x1, Pallas kernels: 12.9 us -> 12.4 us  [local(): pl.pallas_call(functools.partial(kernel, cols, parts, capacity), out_shap...]
where the time goes in v6:
time: 13.2 us; the launch traced here: 13 us
  Pallas kernels  12.4 us (94%)
  local copies, waits for them, and re-layouts  0.63 us (5%)
    pallas_call x1, Pallas kernels, local(): pl.pallas_call(functools.partial(kernel, cols, parts, capacity), out_shap...  12.4 us
    unnamed x1, local copies, waits for them, and re-layouts  0.63 us

profile of v6, /device:TPU:0, one launch (start us, length us, event | category | flops | bytes accessed | tf_op | source)
XLA Modules:
  0.0 13.0 jit_solution(4977121602977976581)
XLA Ops:
  0.0 12.4 %layer.1 = bf16[64,512]{1,0:T(8,128)(2,1)S(1)} custom-call(bf16[192,512]{1,0:T(8,128)(2,1)} %feat_hbm.1, bf16[192,256]{1,0:T(8,128)(2,1)} %proj_hbm.1, bf16[256,256]{1,0:T(8,128)(2,1)} %selfw_hbm.1, bf16[256,256]{1,0:T(8,128)(2,1)} %neighw_hbm.1, s32[16,512]{1,0:T(8,128)} %neigh_hbm.1, s32[1,512]{1,0:T(1,128)} %bitcast.1, s32[1,512]{1,0:T(1,128)} %rows_hbm.1, ...), custom_call_target="tpu_custom_call" | custom-call | tf_op jit(solution)/shard_map/layer/pallas_call | solution.py:388
  12.4 0.6 %copy.10 = bf16[64,512]{1,0:T(8,128)(2,1)} copy(bf16[64,512]{1,0:T(8,128)(2,1)S(1)} %layer.1) | data formatting | bytes 131072

commit v7 on v6

--- a/solution.py
+++ b/solution.py
@@ -140,12 +140,14 @@
         aside(
             fold << stage,
             lambda way, peer: pl.semaphore_signal(
-                known.at[stage, 1 - way], inc=1, device_id=(column, peer), device_id_type=MESH
+                known.at[stage], inc=1, device_id=(column, peer), device_id_type=MESH
             ),
         )
 
     def hear(stage):
-        aside(fold << stage, lambda way, peer: pl.semaphore_wait(known.at[stage, way], 1))
+        distance = fold << stage
+        sides = (part - distance + parts) // parts + 1 - (part + distance) // parts
+        pl.semaphore_wait(known.at[stage], sides)
 
     stages = rounds(pairs)
 
@@ -192,7 +194,7 @@
         return scatter(
             outgoing_self.at[band(peer)],
             incoming_self.at[column],
-            sends.at[1],
+            sends.at[0],
             self_recv.at[0],
             peer,
             part,
@@ -275,13 +277,12 @@
         hear(0)
     if stages > 1:
         tell(1)
-    lax.fori_loop(nodes // depth, counts.shape[0] // depth, tally, 0)
 
     def part_copy(peer, slot):
         return pltpu.make_async_remote_copy(
             src_ref=packed_out.at[peer],
             dst_ref=packed_in.at[slot],
-            send_sem=sends.at[2],
+            send_sem=sends.at[0],
             recv_sem=row_recv.at[slot],
             device_id=(column, peer),
             device_id_type=MESH,
@@ -326,6 +327,7 @@
 
         packed_in[pair] = packed_out[part]
 
+    lax.fori_loop(nodes // depth, counts.shape[0] // depth, tally, 0)
     remote[...] = jnp.zeros((width, nodes), jnp.float32)
 
     def gather(turn, carry):
@@ -346,16 +348,16 @@
         total = total + incoming_self[partner(column, step, cols)].astype(jnp.float32)
     own_self[...] = total
 
-    settle(outgoing_self.at[pl.ds(0, (cols - 1) * width)], sends.at[1])
+    all_sums = cols * width * slots + (cols - 1) * width * nodes
+    carried = all_sums - width * slots + (parts - 1) * width * LANES
 
     @pl.when(part == carrier)
     def _():
-        settle(outgoing_sum.at[:, pl.ds(0, (cols - 1) * width)], sends.at[0])
-        settle(packed_out.at[pl.ds(0, parts - 1)], sends.at[2])
+        settle(counts.at[pl.ds(0, carried // nodes)], sends.at[0])
 
     @pl.when(part != carrier)
     def _():
-        settle(outgoing_sum, sends.at[0])
+        settle(counts.at[pl.ds(0, all_sums // nodes)], sends.at[0])
 
     gather(pairs - 1, 0)
     result = own_self[...] + remote[...] * share
@@ -406,11 +408,11 @@
             pltpu.VMEM((width, nodes), jnp.float32),
             pltpu.VMEM((nodes + slots, nodes), bf16),
             copies((len(arguments),)),
-            copies((3,)),
+            copies((1,)),
             copies((CHUNKS,)),
             copies((parts // fold,)),
             copies((1,)),
-            pltpu.SemaphoreType.REGULAR((max(1, rounds(parts // fold)), 2)),
+            pltpu.SemaphoreType.REGULAR((max(1, rounds(parts // fold)),)),
         ],
         compiler_params=pltpu.CompilerParams(
             collective_id=0, has_side_effects=True, vmem_limit_bytes=limit

time: 13.2 us -> 13.1 us (level)
  no operation moved by 1% of the time
where the time goes in v7:
time: 13.1 us; the launch traced here: 13 us
  Pallas kernels  12.3 us (94%)
  local copies, waits for them, and re-layouts  0.63 us (5%)
    pallas_call x1, Pallas kernels, local(): pl.pallas_call(functools.partial(kernel, cols, parts, capacity), out_shap...  12.3 us
    unnamed x1, local copies, waits for them, and re-layouts  0.63 us

profile of v7, /device:TPU:0, one launch (start us, length us, event | category | flops | bytes accessed | tf_op | source)
XLA Modules:
  0.0 13.0 jit_solution(10834841814522032438)
XLA Ops:
  0.0 12.3 %layer.1 = bf16[64,512]{1,0:T(8,128)(2,1)S(1)} custom-call(bf16[192,512]{1,0:T(8,128)(2,1)} %feat_hbm.1, bf16[192,256]{1,0:T(8,128)(2,1)} %proj_hbm.1, bf16[256,256]{1,0:T(8,128)(2,1)} %selfw_hbm.1, bf16[256,256]{1,0:T(8,128)(2,1)} %neighw_hbm.1, s32[16,512]{1,0:T(8,128)} %neigh_hbm.1, s32[1,512]{1,0:T(1,128)} %bitcast.1, s32[1,512]{1,0:T(1,128)} %rows_hbm.1, ...), custom_call_target="tpu_custom_call" | custom-call | tf_op jit(solution)/shard_map/layer/pallas_call | solution.py:390
  12.3 0.6 %copy.10 = bf16[64,512]{1,0:T(8,128)(2,1)} copy(bf16[64,512]{1,0:T(8,128)(2,1)S(1)} %layer.1) | data formatting | bytes 131072

commit v8 on v7

--- a/solution.py
+++ b/solution.py
@@ -239,8 +239,6 @@
     whole = dot(value, pick[:, lanes:], 1, 0).astype(jnp.bfloat16)
     for chunk in range(1, CHUNKS):
         outgoing_sum[chunk] = whole[:, (chunk - 1) * lanes : chunk * lanes]
-    for chunk in range(1, CHUNKS):
-        sum_start(chunk)
     for load in loads[5:]:
         load.wait()
     weights_self[...] = dot(selfw[...], proj[...], 0, 1).astype(jnp.bfloat16)
@@ -265,7 +263,10 @@
             counts[pl.ds(start, depth), there] = total
         return carry
 
-    lax.fori_loop(0, nodes // depth, tally, 0)
+    lax.fori_loop(0, nodes // depth // 2, tally, 0)
+    for chunk in range(1, CHUNKS):
+        sum_start(chunk)
+    lax.fori_loop(nodes // depth // 2, nodes // depth, tally, 0)
     share = 1.0 / degree[...].astype(jnp.float32)
     value = dot(projected[...], counts[0:nodes, :], 1, 0) * share
     value = value + dot(weights_self[...], feat[...], 1, 0)

time: 13.1 us -> 12.9 us (0.985)
    pallas_call x1, Pallas kernels: 12.3 us -> 12.2 us  [local(): pl.pallas_call(functools.partial(kernel, cols, parts, capacity), out_shap...]
where the time goes in v8:
time: 12.9 us; the launch traced here: 12.8 us
  Pallas kernels  12.2 us (95%)
  local copies, waits for them, and re-layouts  0.63 us (5%)
    pallas_call x1, Pallas kernels, local(): pl.pallas_call(functools.partial(kernel, cols, parts, capacity), out_shap...  12.2 us
    unnamed x1, local copies, waits for them, and re-layouts  0.63 us

profile of v8, /device:TPU:0, one launch (start us, length us, event | category | flops | bytes accessed | tf_op | source)
XLA Modules:
  0.0 12.8 jit_solution(2858710512940053582)
XLA Ops:
  0.0 12.2 %layer.1 = bf16[64,512]{1,0:T(8,128)(2,1)S(1)} custom-call(bf16[192,512]{1,0:T(8,128)(2,1)} %feat_hbm.1, bf16[192,256]{1,0:T(8,128)(2,1)} %proj_hbm.1, bf16[256,256]{1,0:T(8,128)(2,1)} %selfw_hbm.1, bf16[256,256]{1,0:T(8,128)(2,1)} %neighw_hbm.1, s32[16,512]{1,0:T(8,128)} %neigh_hbm.1, s32[1,512]{1,0:T(1,128)} %bitcast.1, s32[1,512]{1,0:T(1,128)} %rows_hbm.1, ...), custom_call_target="tpu_custom_call" | custom-call | tf_op jit(solution)/shard_map/layer/pallas_call | solution.py:391
  12.2 0.6 %copy.10 = bf16[64,512]{1,0:T(8,128)(2,1)} copy(bf16[64,512]{1,0:T(8,128)(2,1)S(1)} %layer.1) | data formatting | bytes 131072

commit v9 on v8

--- a/solution.py
+++ b/solution.py
@@ -222,9 +222,11 @@
             there = slice(chunk * lanes + start, chunk * lanes + start + group)
             pick[:, there] = jnp.where(hit, 1.0, 0.0).astype(jnp.bfloat16)
 
-    for load in loads[:5]:
+    for load in loads[:2]:
         load.wait()
     choose(0)
+    for load in loads[2:5]:
+        load.wait()
     picked = dot(feat[...], pick[:, 0:lanes], 1, 0).astype(jnp.bfloat16)
     turned = dot(neighw[...], proj[...], 0, 1).astype(jnp.bfloat16)
     weights[...] = turned
@@ -264,9 +266,10 @@
         return carry
 
     lax.fori_loop(0, nodes // depth // 2, tally, 0)
-    for chunk in range(1, CHUNKS):
+    for chunk in range(1, CHUNKS - 1):
         sum_start(chunk)
     lax.fori_loop(nodes // depth // 2, nodes // depth, tally, 0)
+    sum_start(CHUNKS - 1)
     share = 1.0 / degree[...].astype(jnp.float32)
     value = dot(projected[...], counts[0:nodes, :], 1, 0) * share
     value = value + dot(weights_self[...], feat[...], 1, 0)

time: 12.9 us -> 13 us (level)
  no operation moved by 1% of the time
where the time goes in v9:
time: 13 us; the launch traced here: 12.8 us
  Pallas kernels  12.2 us (94%)
  local copies, waits for them, and re-layouts  0.63 us (5%)
    pallas_call x1, Pallas kernels, local(): pl.pallas_call(functools.partial(kernel, cols, parts, capacity), out_shap...  12.2 us
    unnamed x1, local copies, waits for them, and re-layouts  0.63 us

profile of v9, /device:TPU:0, one launch (start us, length us, event | category | flops | bytes accessed | tf_op | source)
XLA Modules:
  0.0 12.8 jit_solution(13863033322824444325)
XLA Ops:
  0.0 12.2 %layer.1 = bf16[64,512]{1,0:T(8,128)(2,1)S(1)} custom-call(bf16[192,512]{1,0:T(8,128)(2,1)} %feat_hbm.1, bf16[192,256]{1,0:T(8,128)(2,1)} %proj_hbm.1, bf16[256,256]{1,0:T(8,128)(2,1)} %selfw_hbm.1, bf16[256,256]{1,0:T(8,128)(2,1)} %neighw_hbm.1, s32[16,512]{1,0:T(8,128)} %neigh_hbm.1, s32[1,512]{1,0:T(1,128)} %bitcast.1, s32[1,512]{1,0:T(1,128)} %rows_hbm.1, ...), custom_call_target="tpu_custom_call" | custom-call | tf_op jit(solution)/shard_map/layer/pallas_call | solution.py:394
  12.2 0.6 %copy.10 = bf16[64,512]{1,0:T(8,128)(2,1)} copy(bf16[64,512]{1,0:T(8,128)(2,1)S(1)} %layer.1) | data formatting | bytes 131072
